TPU v7x, 256 devices: a whole 4x4x8 slice. The times are simulated.
256 devices in a mesh: rep: 2 (over core), dp: 128 (over x, y, z).
Axes of the slice: x: 4, y: 4, z: 8, core: 2. Of those that a mesh axis runs over, the one named last changes fastest.
Arguments:
- a: bfloat16 [256, 2, 4096, 768], P(('rep', 'dp')), parts along dimension 0
- g: bfloat16 [256, 2, 4096, 1792], P(('rep', 'dp')), parts along dimension 0
Outputs:
- output: bfloat16 [4, 768, 1792], P('rep'), parts along dimension 0
There are 2 independent parts. A program takes and returns all parts, laid end to end along the dimension named above; each array names one.
All inputs are finite; a program needn't handle non-finite values.
Results may differ from a plain program's by a relative error of at most 0.012.
Values are sent between devices in bfloat16 or wider.
A program may use at most 768 MiB of HBM per device.

v0:
```python
import jax
import jax.numpy as jnp


def solution(mesh):
    groups = mesh.shape["rep"]

    def step(a, g):
        a, g = (t.reshape(groups, -1, *t.shape[1:]) for t in (a, g))
        sums = jnp.einsum("rsntd,rsntf->rndf", a, g, preferred_element_type=jnp.float32)
        return sums.astype(jnp.bfloat16).reshape(-1, *sums.shape[2:])

    return step
```

profile of v0, /device:TPU:0, one launch (start us, length us, event | category | flops | bytes accessed | tf_op | source)
XLA Modules:
  0.0 834.1 jit_solution(6902787718749853157)
XLA Ops:
  0.0 30.4 %fusion.3 = f32[1,2,768,1792]{3,2,1,0:T(8,128)} fusion(bf16[1,2,4096,1792]{3,2,1,0:T(8,128)(2,1)} %param.1, bf16[1,2,4096,768]{3,2,1,0:T(8,128)(2,1)} %param), kind=kOutput, calls=%fused_computation.4 | convolution fusion | flops 22548578304 | bytes 52953088 | tf_op jit(solution)/rsntd,rsntf->rndf/dot_general | solution.py:10
  30.4 803.7 %all-reduce.2 = bf16[1,2,768,1792]{3,2,1,0:T(8,128)(2,1)} all-reduce(f32[1,2,768,1792]{3,2,1,0:T(8,128)} %fusion.3), channel_id=1, replica_groups=[2,128]<=[256], use_global_device_ids=true, to_apply=%add.clone | all-reduce | flops 2752512 | bytes 16515072 | tf_op jit(solution)/rsntd,rsntf->rndf/dot_general | solution.py:10
where the time goes:
time: 834 us
  blocking collectives  804 us (96%)
  matrix products  30.4 us (4%)
    dot_general x1, blocking collectives, step(): jnp.einsum('rsntd,rsntf->rndf', a, g, preferred_element_type=jnp.float32)  804 us
    dot_general x1, matrix products, step(): jnp.einsum('rsntd,rsntf->rndf', a, g, preferred_element_type=jnp.float32)  30.4 us

commit v1 on v0

v1 whole, which is shorter than its diff:
```python
import jax
import jax.numpy as jnp
from jax import lax
from jax.sharding import PartitionSpec as P


def solution(mesh):
    def body(a, g):
        outs = []
        for n in range(2):
            t = lax.dot_general(a[0, n], g[0, n], (((0,), (0,)), ((), ())), preferred_element_type=jnp.float32).astype(jnp.bfloat16)
            outs.append(lax.psum(t, "dp"))
        return jnp.stack(outs)

    return jax.shard_map(body, mesh=mesh, in_specs=(P(("rep", "dp")),) * 2, out_specs=P("rep"), check_vma=False)
```

time: 834 us -> 300 us (0.36)
  the two profiles are of different devices: /device:TPU:0 before, /device:TPU:8 now
where the time goes in v1:
time: 300 us
  waiting for transfers between devices  244 us (81%)
  matrix products  37 us (12%)
  between operations  13.4 us (4%)
  other arithmetic  5.56 us (2%)
    psum x1, waiting for transfers between devices, body(): outs.append(lax.psum(t, 'dp'))  244 us
    dot_general x2, matrix products, body(): lax.dot_general(a[0, n], g[0, n], (((0,), (0,)), ((), ())), preferred_ele...  37 us
  transfers between devices with their start and end apart: 1, of which 1 were waited for; matrix products, arithmetic and copies ran while one was open for 0% of the time, Pallas kernels for 0%

profile of v1, /device:TPU:8, one launch (start us, length us, event | category | flops | bytes accessed | tf_op | source)
XLA Modules:
  0.0 300.2 jit_solution(9052309870204147175)
XLA Ops:
  6.5 0.0 all-reduce.3.cloned.1.call-start
  6.5 0.0 copy-start
  6.5 18.9 %fusion.20 = bf16[1,768,1792]{2,1,0:T(8,128)(2,1)} fusion(bf16[1,2,4096,1792]{3,2,1,0:T(8,128)(2,1)} %param.3, bf16[1,2,4096,768]{3,2,1,0:T(8,128)(2,1)} %param.2), kind=kOutput, calls=%fused_computation.13 | convolution fusion | flops 11275665408 | bytes 23724032 | tf_op jit(solution)/shard_map/dot_general | solution.py:11
  25.4 0.0 copy-done
  25.4 18.1 %fusion.25 = bf16[1,768,1792]{2,1,0:T(8,128)(2,1)} fusion(bf16[1,2,4096,1792]{3,2,1,0:T(8,128)(2,1)} %param.3, bf16[1,2,4096,768]{3,2,1,0:T(8,128)(2,1)S(1)} %copy-done), kind=kOutput, calls=%fused_computation.14 | convolution fusion | flops 11275665408 | bytes 23724032 | tf_op jit(solution)/shard_map/dot_general | solution.py:11
  43.6 0.0 all-reduce.3.cloned.1.call-update
  43.6 244.2 %all-reduce.3.cloned.1.call-done = (bf16[1,768,1792]{2,1,0:T(8,128)(2,1)}, bf16[1,768,1792]{2,1,0:T(8,128)(2,1)}) async-done(((bf16[1,768,1792]{2,1,0:T(8,128)(2,1)}, bf16[1,768,1792]{2,1,0:T(8,128)(2,1)}), (bf16[1,768,1792]{2,1,0:T(8,128)(2,1)}, bf16[1,768,1792]{2,1,0:T(8,128)(2,1)})) %all-reduce.3.cloned.1.call-update) | async-done | bytes 5505040 | tf_op jit(solution)/shard_map/psum | solution.py:12
  287.8 5.6 %pad_maximum_fusion = bf16[2,768,1792]{2,1,0:T(8,128)(2,1)} fusion(bf16[1,768,1792]{2,1,0:T(8,128)(2,1)} %get-tuple-element.5, bf16[1,768,1792]{2,1,0:T(8,128)(2,1)} %get-tuple-element.6), kind=kLoop, calls=%fused_computation.10 | loop fusion | flops 2752512 | bytes 11010048 | tf_op jit(solution)/shard_map/stack | solution.py:13
Async XLA Ops:
  6.5 281.2 %all-reduce.3.cloned.1.call-start = ((), (), s32[]{:S(2)}) async-start(), calls=%async_computation | async-start | bytes 11010048 | tf_op jit(solution)/shard_map/psum | solution.py:12
  6.5 18.9 %copy-start = (bf16[1,2,4096,768]{3,2,1,0:T(8,128)(2,1)S(1)}, bf16[1,2,4096,768]{3,2,1,0:T(8,128)(2,1)}, u32[]{:S(2)}) copy-start(bf16[1,2,4096,768]{3,2,1,0:T(8,128)(2,1)} %param.2) | copy-start | bytes 37748740
Sparse Core Ops, SparseCore 0:
  43.7 244.0 all-reduce.2
